TPU v7x, 32 devices: a whole 2x2x4 slice. The times are simulated.
32 devices in a mesh: dp: 8 (over z, y), mp: 4 (over x, core).
Axes of the slice: x: 2, y: 2, z: 4, core: 2. Of those that a mesh axis runs over, the one named last changes fastest.
Arguments:
- queries: bfloat16 [1024, 8192], P('dp', 'mp'), may hold values from -8 to 8
- tree_keys: bfloat16 [1024, 1024], P('dp', 'mp'), may hold values from -18 to 18
- tree_values: bfloat16 [1024, 1024], P('dp', 'mp'), may hold values from -6 to 6
- cache_keys: bfloat16 [16, 4096, 1024], P('dp', None, 'mp'), may hold values from -8 to 8
- cache_values: bfloat16 [16, 4096, 1024], P('dp', None, 'mp'), may hold values from -6 to 6
- cache_lens: int32 [16], P('dp'), may hold values from 1024 to 4096, as said below
- parents: int32 [16, 64], P('dp'), may hold values from -1 to 62, as said below
- accepted_nodes: int32 [16, 8], P('dp'), may hold values from 0 to 63, as said below
- residual: bfloat16 [1024, 8192], P('dp', 'mp'), may hold values from -1.796875 to 1.796875
- out_weight: bfloat16 [8192, 8192], P('mp', 'dp'), may hold values from -0.0625 to 0.0625
Outputs:
- tree_hidden: bfloat16 [1024, 8192], P('dp', 'mp')
- accepted_hidden: bfloat16 [128, 8192], P(None, 'mp')
Inputs may be any that keep to these rules, and one draw needn't show every extreme that they name: parents[r, 0] = -1 and 0 <= parents[r, i] < i for i >= 1. accepted_nodes[r, 0] = 0, the nodes of a row increase, and parents[r, accepted_nodes[r, a + 1]] = accepted_nodes[r, a]. `cache_lens`: some request has exactly 4096 filled positions.
All inputs are finite; a program needn't handle non-finite values.
Results may differ from a plain program's by a relative error of at most 0.015.
Values may be sent and summed in bfloat16 or wider, within the bound.
A program may use at most 64 MiB of HBM per device.

v0:
```python
import math

import jax
import jax.numpy as jnp
from jax import lax
from jax.sharding import PartitionSpec as P

HEADS = 64
KV_HEADS = 8
HD = 128


neg_large = -1e30


def ancestry(parents, node_count):
    positions = jnp.arange(node_count, dtype=jnp.int32)
    parent_hot = (parents[:, :, None] == positions[None, None, :]).astype(jnp.float32)
    reached = parent_hot + jnp.eye(node_count, dtype=jnp.float32)[None]
    for squaring in range((node_count - 1).bit_length()):
        reached = jnp.minimum(
            jnp.einsum("rij,rjk->rik", reached, reached, precision=lax.Precision.HIGHEST), 1.0
        )
    return reached > 0.5


def per_device(
    queries,
    tree_keys,
    tree_values,
    cache_keys,
    cache_values,
    cache_lens,
    parents,
    accepted_nodes,
    residual,
    out_weight,
):
    request_count = parents.shape[0]
    node_count = parents.shape[1]
    cache_length = cache_keys.shape[1]
    kv_local = tree_keys.shape[1] // HD
    group_size = HEADS // KV_HEADS
    scale_factor = 1.0 / math.sqrt(HD)
    query_grid = queries.reshape(request_count, node_count, kv_local, group_size, HD)
    tree_key_grid = tree_keys.reshape(request_count, node_count, kv_local, HD)
    tree_value_grid = tree_values.reshape(request_count, node_count, kv_local, HD)
    cache_key_grid = cache_keys.reshape(request_count, cache_length, kv_local, HD)
    cache_value_grid = cache_values.reshape(request_count, cache_length, kv_local, HD)
    ancestor = ancestry(parents, node_count)
    tree_scores = (
        jnp.einsum(
            "rnkgd,rjkd->rnkgj", query_grid, tree_key_grid, preferred_element_type=jnp.float32
        )
        * scale_factor
    )
    tree_scores = jnp.where(ancestor[:, :, None, None, :], tree_scores, neg_large)
    run_max = jnp.max(tree_scores, axis=-1)
    tree_weights = jnp.exp(tree_scores - run_max[..., None])
    run_sum = jnp.sum(tree_weights, axis=-1)
    run_acc = jnp.einsum(
        "rnkgj,rjkd->rnkgd",
        tree_weights.astype(jnp.bfloat16),
        tree_value_grid,
        preferred_element_type=jnp.float32,
    )
    block_len = min(512, cache_length)

    def absorb(block_number, state_now):
        old_max, old_sum, old_acc = state_now
        block_start = block_number * block_len
        key_block = lax.dynamic_slice_in_dim(cache_key_grid, block_start, block_len, 1)
        value_block = lax.dynamic_slice_in_dim(cache_value_grid, block_start, block_len, 1)
        block_scores = (
            jnp.einsum(
                "rnkgd,rpkd->rnkgp", query_grid, key_block, preferred_element_type=jnp.float32
            )
            * scale_factor
        )
        positions = block_start + jnp.arange(block_len, dtype=jnp.int32)
        live_keys = positions[None, :] < cache_lens[:, None]
        block_scores = jnp.where(live_keys[:, None, None, None, :], block_scores, neg_large)
        new_max = jnp.maximum(old_max, jnp.max(block_scores, axis=-1))
        block_weights = jnp.exp(block_scores - new_max[..., None])
        rescale = jnp.exp(old_max - new_max)
        new_sum = old_sum * rescale + jnp.sum(block_weights, axis=-1)
        new_acc = old_acc * rescale[..., None] + jnp.einsum(
            "rnkgp,rpkd->rnkgd",
            block_weights.astype(jnp.bfloat16),
            value_block,
            preferred_element_type=jnp.float32,
        )
        return (new_max, new_sum, new_acc)

    trip_count = cache_length // block_len
    run_max, run_sum, run_acc = lax.fori_loop(0, trip_count, absorb, (run_max, run_sum, run_acc))
    attended = (run_acc / run_sum[..., None]).astype(jnp.bfloat16)
    attended = attended.reshape(request_count * node_count, kv_local * group_size * HD)
    feature_share = residual.shape[1]
    all_rows = jnp.dot(
        lax.all_gather(attended, "dp", axis=0, tiled=True),
        out_weight,
        preferred_element_type=jnp.float32,
    )
    partial_sum = lax.all_to_all(
        all_rows.astype(jnp.bfloat16), "dp", split_axis=0, concat_axis=1, tiled=True
    ).astype(all_rows.dtype)
    head_total_sum = lax.psum(partial_sum.astype(jnp.bfloat16), "mp").astype(jnp.float32)
    own_share = lax.dynamic_slice_in_dim(
        head_total_sum, lax.axis_index("mp") * feature_share, feature_share, 1
    )
    tree_hidden = (residual.astype(jnp.float32) + own_share).astype(jnp.bfloat16)
    row_base = jnp.arange(request_count, dtype=jnp.int32)[:, None] * node_count
    picked_rows = (row_base + accepted_nodes).reshape(-1)
    picked_hidden = jnp.take(tree_hidden, picked_rows, axis=0)
    accepted_hidden = lax.all_gather(picked_hidden, "dp", axis=0, tiled=True)
    return (tree_hidden, accepted_hidden)


def solution(mesh):
    placed = (
        P("dp", "mp"),
        P("dp", "mp"),
        P("dp", "mp"),
        P("dp", None, "mp"),
        P("dp", None, "mp"),
        P("dp"),
        P("dp", None),
        P("dp", None),
        P("dp", "mp"),
        P("mp", "dp"),
    )
    return jax.shard_map(
        per_device,
        mesh=mesh,
        in_specs=placed,
        out_specs=(P("dp", "mp"), P(None, "mp")),
        check_vma=False,
    )
```

profile of v0, /device:TPU:0, one launch (start us, length us, event | category | flops | bytes accessed | tf_op | source)
XLA Modules:
  0.0 305.0 jit_solution(8466349382810361783)
XLA Ops:
  13.3 6.4 %copy.23 = bf16[2,4096,256]{1,2,0:T(8,128)(2,1)} copy(bf16[2,4096,256]{2,1,0:T(8,128)(2,1)} %param.15) | data formatting | bytes 8388608 | tf_op args[3]
  19.7 6.4 %copy.24 = bf16[2,4096,256]{1,2,0:T(8,128)(2,1)} copy(bf16[2,4096,256]{2,1,0:T(8,128)(2,1)} %param.16) | data formatting | bytes 8388608 | tf_op args[4]
  26.1 49.3 %while.17 = (s32[]{:T(128)}, f32[2,64,2,8]{1,3,2,0:T(8,128)S(1)}, f32[2,64,2,8]{1,3,2,0:T(8,128)S(1)}, f32[2,64,2,8,128]{4,1,3,2,0:T(8,128)S(1)}, s32[2]{0:T(128...) while((s32[]{:T(128)}, f32[2,64,2,8]{1,3,2,0:T(8,128)S(1)}, ...), condition=%wide.region_5.6_spmd, body=%wide.region_2.5_spmd.sunk | while | flops 548935168 | bytes 16392375 | solution.py:96
  26.2 1.8 bitcast_reduce_fusion.2
  28.0 1.7 fusion.61
  29.7 2.5 fusion.62
  32.3 1.8 bitcast_reduce_fusion.2
  34.2 1.7 fusion.61
  35.9 2.5 fusion.62
  38.5 1.8 bitcast_reduce_fusion.2
  40.3 1.7 fusion.61
  42.1 2.5 fusion.62
  44.7 1.8 bitcast_reduce_fusion.2
  46.5 1.7 fusion.61
  48.2 2.5 fusion.62
  50.8 1.8 bitcast_reduce_fusion.2
  52.7 1.7 fusion.61
  54.4 2.5 fusion.62
  57.0 1.8 bitcast_reduce_fusion.2
  58.9 1.7 fusion.61
  60.6 2.5 fusion.62
  63.2 1.8 bitcast_reduce_fusion.2
  65.0 1.7 fusion.61
  66.7 2.5 fusion.62
  69.3 1.8 bitcast_reduce_fusion.2
  71.2 1.7 fusion.61
  72.9 2.5 fusion.62
  77.2 75.6 %all-gather.2.cloned.1.call-done = bf16[1024,2048]{1,0:T(8,128)(2,1)} async-done(((bf16[128,2048]{1,0:T(8,128)(2,1)}), bf16[1024,2048]{1,0:T(8,128)(2,1)}) %all-gather.2.cloned.1.call-update) | async-done | bytes 4194320 | tf_op jit(solution)/shard_map/all_gather | solution.py:101
  152.8 7.9 %convolution_convert_fusion = bf16[1024,1024]{1,0:T(8,128)(2,1)S(1)} fusion(bf16[1024,2048]{1,0:T(8,128)(2,1)} %all-gather.2.cloned.1.call-done, bf16[2048,1024]{1,0:T(8,128)(2,1)} %param.21), kind=kOutput, calls=%fused_computation.27 | convolution fusion | flops 4296015872 | bytes 10485760 | tf_op jit(solution)/shard_map/dot_general | solution.py:100
  160.8 51.1 %all_to_all.19 = bf16[8,128,1024]{2,1,0:T(8,128)(2,1)S(1)} all-to-all(bf16[8,128,1024]{2,1,0:T(8,128)(2,1)S(1)} %bitcast.87), channel_id=1, replica_groups=mesh['dp'=8,'mp'=4] {'dp'}, dimensions={0} | all-to-all | bytes 4194304 | tf_op jit(solution)/shard_map/all_to_all | solution.py:105
  213.7 50.2 %all-reduce.2.cloned.1.call-done = bf16[128,8192]{1,0:T(8,128)(2,1)} async-done(((bf16[128,8192]{1,0:T(8,128)(2,1)}), bf16[128,8192]{1,0:T(8,128)(2,1)}) %all-reduce.2.cloned.1.call-update) | async-done | bytes 2097168 | tf_op jit(solution)/shard_map/psum | solution.py:108
  265.7 31.6 %all_gather.7 = bf16[128,2048]{1,0:T(8,128)(2,1)S(1)} all-gather(bf16[16,2048]{1,0:T(8,128)(2,1)S(1)} %broadcast_select_fusion), channel_id=1, replica_groups=mesh['dp'=8,'mp'=4] {'dp'}, dimensions={0}, use_global_device_ids=true | all-gather | bytes 589824 | tf_op jit(solution)/shard_map/all_gather | solution.py:116
  (86 shorter events, 13.0 us)
Async XLA Ops:
  7.2 5.6 %copy-start.2 = (bf16[128,256]{1,0:T(8,128)(2,1)S(1)}, bf16[128,256]{1,0:T(8,128)(2,1)}, u32[]{:S(2)}) copy-start(bf16[128,256]{1,0:T(8,128)(2,1)} %param.14) | copy-start | bytes 196612
  7.2 145.7 %all-gather.2.cloned.1.call-start = ((), (), s32[]{:S(2)}) async-start(), calls=%async_computation.1 | async-start | bytes 4718592 | tf_op jit(solution)/shard_map/all_gather | solution.py:101
  19.7 6.4 %copy-start.3 = (s32[2]{0:T(128)S(1)}, s32[2]{0:T(128)}, u32[]{:S(2)}) copy-start(s32[2]{0:T(128)} %param.17) | copy-start | bytes 28
  77.2 186.7 %all-reduce.2.cloned.1.call-start = ((), (), s32[]{:S(2)}) async-start(), calls=%async_computation.2 | async-start | bytes 4194304 | tf_op jit(solution)/shard_map/psum | solution.py:108
  211.9 1.5 copy-start.4
  211.9 51.9 %copy-start.1 = (bf16[128,2048]{1,0:T(8,128)(2,1)S(1)}, bf16[128,2048]{1,0:T(8,128)(2,1)}, u32[]{:S(2)}) copy-start(bf16[128,2048]{1,0:T(8,128)(2,1)} %param.20) | copy-start | bytes 1572868
  265.1 33.1 %copy-start = (bf16[128,2048]{1,0:T(8,128)(2,1)}, bf16[128,2048]{1,0:T(8,128)(2,1)S(1)}, u32[]{:S(2)}) copy-start(bf16[128,2048]{1,0:T(8,128)(2,1)S(1)} %add_convert_fusion) | copy-start | bytes 1572868
Sparse Core Ops, SparseCore 0:
  77.3 75.5 all-gather.1
  213.5 50.2 all-reduce.1
where the time goes:
time: 306 us; the launch traced here: 305 us
  waiting for transfers between devices  126 us (41%)
  blocking collectives  82.7 us (27%)
  matrix products  45.3 us (15%)
  local copies, waits for them, and re-layouts  20 us (7%)
  other arithmetic  16.3 us (5%)
  between operations  14.2 us (5%)
    all_gather x1, waiting for transfers between devices, per_device(): lax.all_gather(attended, 'dp', axis=0, tiled=True)  75.6 us
    all_to_all x1, blocking collectives, per_device(): lax.all_to_all(all_rows.astype(jnp.bfloat16), 'dp', split_axis=0, concat_...  51.1 us
    psum x1, waiting for transfers between devices, per_device(): lax.psum(partial_sum.astype(jnp.bfloat16), 'mp').astype(jnp.float32)  50.2 us
    all_gather x1, blocking collectives, per_device(): accepted_hidden = lax.all_gather(picked_hidden, 'dp', axis=0, tiled=True)  31.6 us
    dot_general x8, matrix products, absorb(): jnp.einsum('rnkgp,rpkd->rnkgd', block_weights.astype(jnp.bfloat16), value...  19.8 us
    unnamed x14, local copies, waits for them, and re-layouts  14.7 us
    dot_general x8, matrix products, absorb(): jnp.einsum('rnkgd,rpkd->rnkgp', query_grid, key_block, preferred_element_...  14.7 us
    reduce_sum x8, other arithmetic, absorb(): new_sum = old_sum * rescale + jnp.sum(block_weights, axis=-1)  13.6 us
  transfers between devices with their start and end apart: 2, of which 2 were waited for; matrix products, arithmetic and copies ran while one was open for 0% of the time, Pallas kernels for 0%

commit v1 on v0

v1 whole, which is shorter than its diff:
```python
import functools
import math

import jax
import jax.numpy as jnp
from jax import lax
from jax.experimental import pallas as pl
from jax.experimental.pallas import tpu as pltpu
from jax.sharding import PartitionSpec as P

HEADS = 64
KV_HEADS = 8
HD = 128
neg_large = -1e30
MESH = pl.DeviceIdType.MESH


def attention_kernel(lens_ref, q_ref, tk_ref, tv_ref, ck_ref, cv_ref, par_ref, o_ref):
    nodes = tk_ref.shape[0]
    cache = ck_ref.shape[1]
    group = q_ref.shape[1] // HD
    block = min(1024, cache)
    factor = math.log2(math.e) / math.sqrt(HD)
    f32 = jnp.float32
    bf = jnp.bfloat16
    length = lens_ref[pl.program_id(0)]

    lane = lax.broadcasted_iota(jnp.int32, (nodes, nodes), 1)
    row = lax.broadcasted_iota(jnp.int32, (nodes, nodes), 0)
    reached = jnp.where((par_ref[0] == lane) | (row == lane), 1.0, 0.0).astype(f32)
    for _ in range((nodes - 1).bit_length()):
        hot = reached.astype(bf)
        reached = jnp.minimum(jnp.dot(hot, hot, preferred_element_type=f32), 1.0)

    parts = 2
    per = group // parts
    rows = per * nodes
    nt = (((1,), (1,)), ((), ()))

    def queries(p):
        return jnp.concatenate(
            [q_ref[:, (p * per + g) * HD : (p * per + g + 1) * HD] for g in range(per)], axis=0
        )

    def with_ones(v):
        return jnp.concatenate([v, jnp.ones(v.shape, bf)], axis=1)

    mask = jnp.concatenate([reached] * per, axis=0) > 0.5
    state = []
    for p in range(parts):
        s = lax.dot_general(queries(p), tk_ref[...], nt, preferred_element_type=f32)
        s = jnp.where(mask, s, neg_large)
        m = jnp.max(s, axis=1, keepdims=True)
        w = jnp.exp2((s - m) * factor).astype(bf)
        acc = jnp.dot(w, with_ones(tv_ref[...]), preferred_element_type=f32)
        state += [m, acc]

    def step(b, state, masked):
        start = pl.multiple_of(b * block, block)
        k = ck_ref[0, pl.ds(start, block), :]
        v = with_ones(cv_ref[0, pl.ds(start, block), :])
        out = []
        scores = [
            lax.dot_general(queries(p), k, nt, preferred_element_type=f32) for p in range(parts)
        ]
        for p in range(parts):
            m, acc = state[2 * p], state[2 * p + 1]
            s = scores[p]
            if masked:
                at = start + lax.broadcasted_iota(jnp.int32, (1, block), 1)
                s = jnp.where(at < length, s, neg_large)
            new = jnp.maximum(m, jnp.max(s, axis=1, keepdims=True))
            w = jnp.exp2((s - new) * factor).astype(bf)
            acc = acc * jnp.exp2((m - new) * factor) + jnp.dot(w, v, preferred_element_type=f32)
            out += [new, acc]
        return tuple(out)

    full = length // block
    state = lax.fori_loop(0, full, lambda b, c: step(b, c, False), tuple(state))
    state = lax.fori_loop(full, pl.cdiv(length, block), lambda b, c: step(b, c, True), state)
    for p in range(parts):
        acc = state[2 * p + 1]
        done = (acc[:, :HD] / acc[:, HD:]).astype(bf)
        for g in range(per):
            o_ref[:, (p * per + g) * HD : (p * per + g + 1) * HD] = done[
                g * nodes : (g + 1) * nodes
            ]


def attend(queries, tree_keys, tree_values, cache_keys, cache_values, cache_lens, parents):
    requests, nodes = parents.shape
    cache = cache_keys.shape[1]
    kv = tree_keys.shape[1] // HD
    wide = queries.shape[1] // kv
    return pl.pallas_call(
        attention_kernel,
        out_shape=jax.ShapeDtypeStruct(queries.shape, jnp.bfloat16),
        grid_spec=pltpu.PrefetchScalarGridSpec(
            num_scalar_prefetch=1,
            grid=(requests, kv),
            in_specs=[
                pl.BlockSpec((nodes, wide), lambda r, k, _: (r, k)),
                pl.BlockSpec((nodes, HD), lambda r, k, _: (r, k)),
                pl.BlockSpec((nodes, HD), lambda r, k, _: (r, k)),
                pl.BlockSpec((1, cache, HD), lambda r, k, _: (r, 0, k)),
                pl.BlockSpec((1, cache, HD), lambda r, k, _: (r, 0, k)),
                pl.BlockSpec((1, nodes, 1), lambda r, k, _: (r, 0, 0)),
            ],
            out_specs=pl.BlockSpec((nodes, wide), lambda r, k, _: (r, k)),
        ),
        compiler_params=pltpu.CompilerParams(vmem_limit_bytes=40 * 1024 * 1024),
        name="attention",
    )(cache_lens, queries, tree_keys, tree_values, cache_keys, cache_values, parents[:, :, None])


def per_device(
    queries,
    tree_keys,
    tree_values,
    cache_keys,
    cache_values,
    cache_lens,
    parents,
    accepted_nodes,
    residual,
    out_weight,
):
    request_count, node_count = parents.shape
    attended = attend(
        queries, tree_keys, tree_values, cache_keys, cache_values, cache_lens, parents
    )
    feature_share = residual.shape[1]
    all_rows = jnp.dot(
        lax.all_gather(attended, "dp", axis=0, tiled=True),
        out_weight,
        preferred_element_type=jnp.float32,
    )
    partial_sum = lax.all_to_all(
        all_rows.astype(jnp.bfloat16), "dp", split_axis=0, concat_axis=1, tiled=True
    ).astype(all_rows.dtype)
    head_total_sum = lax.psum(partial_sum.astype(jnp.bfloat16), "mp").astype(jnp.float32)
    own_share = lax.dynamic_slice_in_dim(
        head_total_sum, lax.axis_index("mp") * feature_share, feature_share, 1
    )
    tree_hidden = (residual.astype(jnp.float32) + own_share).astype(jnp.bfloat16)
    row_base = jnp.arange(request_count, dtype=jnp.int32)[:, None] * node_count
    picked_rows = (row_base + accepted_nodes).reshape(-1)
    picked_hidden = jnp.take(tree_hidden, picked_rows, axis=0)
    accepted_hidden = lax.all_gather(picked_hidden, "dp", axis=0, tiled=True)
    return (tree_hidden, accepted_hidden)


def solution(mesh):
    placed = (
        P("dp", "mp"),
        P("dp", "mp"),
        P("dp", "mp"),
        P("dp", None, "mp"),
        P("dp", None, "mp"),
        P("dp"),
        P("dp", None),
        P("dp", None),
        P("dp", "mp"),
        P("mp", "dp"),
    )
    return jax.shard_map(
        per_device,
        mesh=mesh,
        in_specs=placed,
        out_specs=(P("dp", "mp"), P(None, "mp")),
        check_vma=False,
    )
```

time: 306 us -> 268 us (0.88)
  matrix products: 45.3 us -> 7.95 us
  Pallas kernels: 0 us -> 23.1 us
  other arithmetic: 16.3 us -> 1.34 us
  local copies, waits for them, and re-layouts: 20 us -> 11.6 us
    dot_general x24 -> x0, matrix products: 37.3 us -> none  [the longest x8 19.8 us: absorb(): jnp.einsum('rnkgp,rpkd->rnkgd', block_weights.astype(jnp.bfloat16), value...]
    pallas_call x0 -> x1, Pallas kernels: none -> 23.1 us  [attend(): pl.pallas_call(attention_kernel, out_shape=jax.ShapeDtypeStruct(queries.s...]
    reduce_sum x8 -> x0, other arithmetic: 13.6 us -> none  [absorb(): new_sum = old_sum * rescale + jnp.sum(block_weights, axis=-1)]
    unnamed x14 -> x19, local copies, waits for them, and re-layouts: 14.7 us -> 8.55 us
where the time goes in v1:
time: 268 us; the launch traced here: 266 us
  waiting for transfers between devices  125 us (47%)
  blocking collectives  82.7 us (31%)
  Pallas kernels  23.1 us (9%)
  between operations  14.1 us (5%)
  local copies, waits for them, and re-layouts  11.6 us (4%)
  matrix products  7.95 us (3%)
    all_gather x1, waiting for transfers between devices, per_device(): lax.all_gather(attended, 'dp', axis=0, tiled=True)  74.7 us
    all_to_all x1, blocking collectives, per_device(): lax.all_to_all(all_rows.astype(jnp.bfloat16), 'dp', split_axis=0, concat_...  51.1 us
    psum x1, waiting for transfers between devices, per_device(): lax.psum(partial_sum.astype(jnp.bfloat16), 'mp').astype(jnp.float32)  50.2 us
    all_gather x1, blocking collectives, per_device(): accepted_hidden = lax.all_gather(picked_hidden, 'dp', axis=0, tiled=True)  31.6 us
    pallas_call x1, Pallas kernels, attend(): pl.pallas_call(attention_kernel, out_shape=jax.ShapeDtypeStruct(queries.s...  23.1 us
    unnamed x19, local copies, waits for them, and re-layouts  8.55 us
    dot_general x1, matrix products, per_device(): jnp.dot(lax.all_gather(attended, 'dp', axis=0, tiled=True), out_weight, p...  7.95 us
  transfers between devices with their start and end apart: 2, of which 2 were waited for; matrix products, arithmetic and copies ran while one was open for 0% of the time, Pallas kernels for 0%

profile of v1, /device:TPU:0, one launch (start us, length us, event | category | flops | bytes accessed | tf_op | source)
XLA Modules:
  0.0 265.7 jit_solution(2399193024081033160)
XLA Ops:
  7.2 0.0 all-gather.2.cloned.1.call-start
  7.2 0.8 copy.12.par_ref
  8.0 0.0 copy-start
  8.0 2.2 copy-done
  10.2 0.0 copy-start.1
  10.2 2.2 copy-done.1
  12.4 0.0 copy-start.2
  12.4 1.0 copy-done.2
  13.4 0.8 copy-done.3
  14.3 0.8 copy-done.4
  15.1 0.7 copy-done.5
  15.8 23.1 %attention.1 = bf16[128,2048]{1,0:T(8,128)(2,1)} custom-call(s32[2]{0:T(128)S(1)} %copy-done.5, bf16[128,2048]{1,0:T(8,128)(2,1)S(1)} %copy-done.2, bf16[128,256]{1,0:T(8,128)(2,1)S(1)} %copy-done.3, bf16[128,256]{1,0:T(8,128)(2,1)S(1)} %copy-done.4, bf16[2,4096,256]{2,1,0:T(8,128)(2,1)S(1)} %copy-done, bf16[2,4096,256]{2,1,0:T(8,128)(2,1)S(1)} %copy-done.1, ...), custom_call_target="tpu_custom_call" | custom-call | tf_op jit(solution)/shard_map/attention/pallas_call | solution.py:95
  38.8 0.0 all-gather.2.cloned.1.call-update
  38.9 0.0 all-reduce.2.cloned.1.call-start
  38.9 74.7 %all-gather.2.cloned.1.call-done = bf16[1024,2048]{1,0:T(8,128)(2,1)} async-done(((bf16[128,2048]{1,0:T(8,128)(2,1)}), bf16[1024,2048]{1,0:T(8,128)(2,1)}) %all-gather.2.cloned.1.call-update) | async-done | bytes 4194320 | tf_op jit(solution)/shard_map/all_gather | solution.py:134
  113.6 7.9 %convolution_convert_fusion = bf16[1024,1024]{1,0:T(8,128)(2,1)S(1)} fusion(bf16[1024,2048]{1,0:T(8,128)(2,1)} %all-gather.2.cloned.1.call-done, bf16[2048,1024]{1,0:T(8,128)(2,1)} %param.19), kind=kOutput, calls=%fused_computation.1 | convolution fusion | flops 4296015872 | bytes 10485760 | tf_op jit(solution)/shard_map/dot_general | solution.py:133
  121.5 51.1 %all_to_all.19 = bf16[8,128,1024]{2,1,0:T(8,128)(2,1)S(1)} all-to-all(bf16[8,128,1024]{2,1,0:T(8,128)(2,1)S(1)} %bitcast.11), channel_id=1, replica_groups=mesh['dp'=8,'mp'=4] {'dp'}, dimensions={0} | all-to-all | bytes 4194304 | tf_op jit(solution)/shard_map/all_to_all | solution.py:138
  172.7 1.5 copy.14
  174.2 0.0 all-reduce.2.cloned.1.call-update
  174.2 0.0 copy-done.8
  174.2 0.1 broadcast_add_fusion
  174.3 0.1 reshape.52
  174.4 0.1 reshape.51
  174.5 50.2 %all-reduce.2.cloned.1.call-done = bf16[128,8192]{1,0:T(8,128)(2,1)} async-done(((bf16[128,8192]{1,0:T(8,128)(2,1)}), bf16[128,8192]{1,0:T(8,128)(2,1)}) %all-reduce.2.cloned.1.call-update) | async-done | bytes 2097168 | tf_op jit(solution)/shard_map/psum | solution.py:141
  224.6 0.0 copy-done.7
  224.6 1.2 add_convert_fusion
  225.8 0.0 copy-start.6
  225.8 0.6 gather_fusion
  226.4 0.1 broadcast_select_fusion
  226.5 31.6 %all_gather.7 = bf16[128,2048]{1,0:T(8,128)(2,1)S(1)} all-gather(bf16[16,2048]{1,0:T(8,128)(2,1)S(1)} %broadcast_select_fusion), channel_id=1, replica_groups=mesh['dp'=8,'mp'=4] {'dp'}, dimensions={0}, use_global_device_ids=true | all-gather | bytes 589824 | tf_op jit(solution)/shard_map/all_gather | solution.py:149
  258.1 0.8 copy.17
  258.9 0.0 copy-done.6
  (9 shorter events, 0.0 us)
Async XLA Ops:
  7.2 106.4 %all-gather.2.cloned.1.call-start = ((), (), s32[]{:S(2)}) async-start(), calls=%async_computation.1 | async-start | bytes 4718592 | tf_op jit(solution)/shard_map/all_gather | solution.py:134
  8.0 2.2 copy-start
  10.2 2.2 copy-start.1
  12.4 1.0 copy-start.2
  13.4 0.8 copy-start.3
  14.3 0.8 copy-start.4
  15.1 0.7 copy-start.5
  38.9 185.8 %all-reduce.2.cloned.1.call-start = ((), (), s32[]{:S(2)}) async-start(), calls=%async_computation.2 | async-start | bytes 4194304 | tf_op jit(solution)/shard_map/psum | solution.py:141
  172.7 1.5 copy-start.8
  172.7 52.0 %copy-start.7 = (bf16[128,2048]{1,0:T(8,128)(2,1)S(1)}, bf16[128,2048]{1,0:T(8,128)(2,1)}, u32[]{:S(2)}) copy-start(bf16[128,2048]{1,0:T(8,128)(2,1)} %param.18) | copy-start | bytes 1572868
  225.8 33.1 %copy-start.6 = (bf16[128,2048]{1,0:T(8,128)(2,1)}, bf16[128,2048]{1,0:T(8,128)(2,1)S(1)}, u32[]{:S(2)}) copy-start(bf16[128,2048]{1,0:T(8,128)(2,1)S(1)} %add_convert_fusion) | copy-start | bytes 1572868
Sparse Core Ops, SparseCore 0:
  39.0 74.5 all-gather.1
  174.3 50.2 all-reduce.1

commit v2 on v1

--- a/solution.py
+++ b/solution.py
@@ -113,7 +113,285 @@
     )(cache_lens, queries, tree_keys, tree_values, cache_keys, cache_values, parents[:, :, None])
 
 
+def line_order(place, length, event):
+    short = jnp.minimum(place, length - 1 - place)
+    ring = (event + 1) // 2
+    near = jnp.where(event % 2 == 1, place - ring, place + ring)
+    far = jnp.where(place < length - 1 - place, event, length - 1 - event)
+    return jnp.where(event <= 2 * short, near, far)
+
+
+def project_kernel(
+    dp_size,
+    mp_size,
+    att_ref,
+    w_ref,
+    res_ref,
+    pick_ref,
+    hid_ref,
+    acc_ref,
+    gathered,
+    total,
+    *rest,
+):
+    f32, bf = jnp.float32, jnp.bfloat16
+    stages = (mp_size - 1).bit_length()
+    outgoing, incoming = rest[:stages], rest[stages : 2 * stages]
+    (
+        settled, owned, picks,
+        ga_send, ga_recv, st_send, st_recv, own_send, own_recv, pk_send, pk_recv,
+    ) = rest[2 * stages :]
+    rows = att_ref.shape[0]
+    wide = w_ref.shape[1]
+    share = dp_size // mp_size
+    length = dp_size // 2
+    d = lax.axis_index("dp")
+    m = lax.axis_index("mp")
+    place, side = d // 2, d % 2
+    peer_side = 1 - side
+
+    barrier = pltpu.get_barrier_semaphore()
+
+    def greet(i, carry):
+        @pl.when(i != d * mp_size + m)
+        def _():
+            pl.semaphore_signal(
+                barrier, inc=1, device_id=(i // mp_size, i % mp_size), device_id_type=MESH
+            )
+
+        return carry
+
+    lax.fori_loop(0, dp_size * mp_size, greet, 0)
+    pl.semaphore_wait(barrier, dp_size * mp_size - 1)
+
+    def gather_copy(src, j, way, target):
+        return pltpu.make_async_remote_copy(
+            src_ref=src,
+            dst_ref=gathered.at[j],
+            send_sem=ga_send.at[j, way],
+            recv_sem=ga_recv.at[j],
+            device_id=(target, m),
+            device_id_type=MESH,
+        )
+
+    def spread(src, j, at, started):
+        up = place + 1
+        down = place - 1
+        for way, ok, target in (
+            (0, (at <= place) & (up < length), up * 2 + side),
+            (1, (at >= place) & (down >= 0), down * 2 + side),
+        ):
+
+            @pl.when(ok)
+            def _():
+                copy = gather_copy(src, j, way, target)
+                copy.start() if started else copy.wait_send()
+
+        copy = gather_copy(src, j, 2, place * 2 + peer_side)
+        copy.start() if started else copy.wait_send()
+
+    def stage_copy(t, j):
+        bit = 1 << t
+        partner = m + bit * (1 - 2 * ((m // bit) % 2))
+        return pltpu.make_async_remote_copy(
+            src_ref=outgoing[t].at[j],
+            dst_ref=incoming[t].at[j],
+            send_sem=st_send.at[t, j],
+            recv_sem=st_recv.at[t, j],
+            device_id=(d, partner),
+            device_id_type=MESH,
+        )
+
+    def kept(t):
+        offset = 0
+        for u in range(t):
+            offset = offset + ((m // (1 << u)) % 2) * (rows >> (u + 1))
+        return offset
+
+    def half(t, keep):
+        bit = (m // (1 << t)) % 2
+        pick = bit if keep else 1 - bit
+        size = rows >> (t + 1)
+        return pl.ds(pl.multiple_of(kept(t) + pick * size, 16), size)
+
+    def push(t, j):
+        outgoing[t][j] = total[j, half(t, False), :].astype(bf)
+        stage_copy(t, j).start()
+
+    final = rows >> stages
+    tile = min(512, wide)
+
+    def multiply(src, j):
+        @pl.loop(0, wide // tile)
+        def _(n):
+            cols = pl.ds(pl.multiple_of(n * tile, tile), tile)
+            total[j, :, cols] = jnp.dot(src[...], w_ref[:, cols], preferred_element_type=f32)
+
+        push(0, j)
+
+    def final_copy(j):
+        return pltpu.make_async_remote_copy(
+            src_ref=settled.at[j],
+            dst_ref=owned.at[d % share, m],
+            send_sem=own_send.at[j],
+            recv_sem=own_recv.at[d % share, m],
+            device_id=(j, d // share),
+            device_id_type=MESH,
+        )
+
+    def final_local(j):
+        return pltpu.make_async_copy(
+            settled.at[j], owned.at[d % share, m], own_recv.at[d % share, m]
+        )
+
+    def fold(t, j):
+        stage_copy(t, j).wait_recv()
+        keep = half(t, True)
+        if t + 1 < stages:
+            total[j, keep, :] = total[j, keep, :] + incoming[t][j].astype(f32)
+            push(t + 1, j)
+        else:
+            settled[j] = (total[j, keep, :] + incoming[t][j].astype(f32)).astype(bf)
+            own = (j == d) & (d // share == m)
+
+            @pl.when(own)
+            def _():
+                final_local(j).start()
+
+            @pl.when(jnp.logical_not(own))
+            def _():
+                final_copy(j).start()
+
+    def own_block(e):
+        return line_order(place, length, e) * 2 + side
+
+    def peer_block(e):
+        return line_order(place, length, e) * 2 + peer_side
+
+    def block_at(k):
+        if k == 0:
+            return own_block(0)
+        if k == dp_size - 1:
+            return peer_block(length - 1)
+        return own_block((k + 1) // 2) if k % 2 == 1 else peer_block(k // 2 - 1)
+
+    spread(att_ref, d, place, True)
+    for k in range(dp_size + stages):
+        if k < dp_size:
+            j = block_at(k)
+            if k == 0:
+                multiply(att_ref, j)
+            else:
+                gather_copy(gathered.at[j], j, 2, d * 0 + place * 2 + peer_side).wait_recv()
+                if k % 2 == 1 and k < dp_size - 1:
+                    spread(gathered.at[j], j, j // 2, True)
+                multiply(gathered.at[j], j)
+        for t in range(stages):
+            b = k - 1 - t
+            if 0 <= b < dp_size:
+                fold(t, block_at(b))
+
+    for i in range(share):
+        cols = slice(i * wide, (i + 1) * wide)
+        for p in range(mp_size):
+            pltpu.make_async_copy(settled.at[0], owned.at[i, p], own_recv.at[i, p]).wait()
+            start = 0
+            for t in range(stages):
+                start += ((p >> t) & 1) * (rows >> (t + 1))
+            at = slice(start, start + final)
+            hid_ref[at, cols] = (res_ref[at, cols].astype(f32) + owned[i, p].astype(f32)).astype(bf)
+
+    count = pick_ref.shape[0]
+    hot = pick_ref[...] == lax.broadcasted_iota(jnp.int32, (count, rows), 1)
+    picked = jnp.dot(
+        jnp.where(hot, 1.0, 0.0).astype(bf), hid_ref[...], preferred_element_type=f32
+    ).astype(bf)
+    picks[d] = picked
+
+    def pick_copy(step):
+        target = lax.rem(d + step, dp_size)
+        return pltpu.make_async_remote_copy(
+            src_ref=picks.at[d],
+            dst_ref=picks.at[d],
+            send_sem=pk_send.at[step],
+            recv_sem=pk_recv.at[d],
+            device_id=(target, m),
+            device_id_type=MESH,
+        )
+
+    def pick_wait(step):
+        source = lax.rem(d + step, dp_size)
+        pltpu.make_async_copy(picks.at[source], picks.at[source], pk_recv.at[source]).wait()
+
+    for step in range(1, dp_size):
+        pick_copy(step).start()
+    spread(att_ref, d, place, False)
+    for e in range(1, length):
+        j = own_block(e)
+        spread(gathered.at[j], j, j // 2, False)
+    for j in range(dp_size):
+        for t in range(stages):
+            stage_copy(t, j).wait_send()
+
+        @pl.when(jnp.logical_not((j == d) & (d // share == m)))
+        def _():
+            final_copy(j).wait_send()
+
+    acc_ref[pl.ds(pl.multiple_of(d * count, count), count), :] = picked
+    for step in range(1, dp_size):
+        pick_wait(step)
+        source = lax.rem(d + step, dp_size)
+        acc_ref[pl.ds(pl.multiple_of(source * count, count), count), :] = picks[source]
+    for step in range(1, dp_size):
+        pick_copy(step).wait_send()
+
+
+def project(attended, out_weight, residual, picks, dp_size, mp_size):
+    bf = jnp.bfloat16
+    rows, depth = attended.shape
+    wide = out_weight.shape[1]
+    features = residual.shape[1]
+    count = picks.shape[0]
+    stages = (mp_size - 1).bit_length()
+    share = dp_size // mp_size
+    halves = [pltpu.VMEM((dp_size, rows >> (t + 1), wide), bf) for t in range(stages)]
+    dma = pltpu.SemaphoreType.DMA
+    vmem = pl.BlockSpec(memory_space=pltpu.VMEM)
+    return pl.pallas_call(
+        functools.partial(project_kernel, dp_size, mp_size),
+        out_shape=(
+            jax.ShapeDtypeStruct((rows, features), bf),
+            jax.ShapeDtypeStruct((dp_size * count, features), bf),
+        ),
+        in_specs=[vmem] * 4,
+        out_specs=(vmem, vmem),
+        scratch_shapes=[
+            pltpu.VMEM((dp_size, rows, depth), bf),
+            pltpu.VMEM((dp_size, rows, wide), jnp.float32),
+            *halves,
+            *halves,
+            pltpu.VMEM((dp_size, rows >> stages, wide), bf),
+            pltpu.VMEM((share, mp_size, rows >> stages, wide), bf),
+            pltpu.VMEM((dp_size, count, features), bf),
+            dma((dp_size, 3)),
+            dma((dp_size,)),
+            dma((stages, dp_size)),
+            dma((stages, dp_size)),
+            dma((dp_size,)),
+            dma((share, mp_size)),
+            dma((dp_size,)),
+            dma((dp_size,)),
+        ],
+        compiler_params=pltpu.CompilerParams(
+            collective_id=0, has_side_effects=True, vmem_limit_bytes=56 * 1024 * 1024
+        ),
+        name="project",
+    )(attended, out_weight, residual, picks)
+
+
 def per_device(
+    dp_size,
+    mp_size,
     queries,
     tree_keys,
     tree_values,
@@ -129,25 +407,9 @@
     attended = attend(
         queries, tree_keys, tree_values, cache_keys, cache_values, cache_lens, parents
     )
-    feature_share = residual.shape[1]
-    all_rows = jnp.dot(
-        lax.all_gather(attended, "dp", axis=0, tiled=True),
-        out_weight,
-        preferred_element_type=jnp.float32,
-    )
-    partial_sum = lax.all_to_all(
-        all_rows.astype(jnp.bfloat16), "dp", split_axis=0, concat_axis=1, tiled=True
-    ).astype(all_rows.dtype)
-    head_total_sum = lax.psum(partial_sum.astype(jnp.bfloat16), "mp").astype(jnp.float32)
-    own_share = lax.dynamic_slice_in_dim(
-        head_total_sum, lax.axis_index("mp") * feature_share, feature_share, 1
-    )
-    tree_hidden = (residual.astype(jnp.float32) + own_share).astype(jnp.bfloat16)
     row_base = jnp.arange(request_count, dtype=jnp.int32)[:, None] * node_count
-    picked_rows = (row_base + accepted_nodes).reshape(-1)
-    picked_hidden = jnp.take(tree_hidden, picked_rows, axis=0)
-    accepted_hidden = lax.all_gather(picked_hidden, "dp", axis=0, tiled=True)
-    return (tree_hidden, accepted_hidden)
+    picks = (row_base + accepted_nodes).reshape(-1, 1)
+    return project(attended, out_weight, residual, picks, dp_size, mp_size)
 
 
 def solution(mesh):
@@ -164,7 +426,7 @@
         P("mp", "dp"),
     )
     return jax.shard_map(
-        per_device,
+        functools.partial(per_device, mesh.shape["dp"], mesh.shape["mp"]),
         mesh=mesh,
         in_specs=placed,
         out_specs=(P("dp", "mp"), P(None, "mp")),

time: 268 us -> 126 us (0.47)
  waiting for transfers between devices: 125 us -> 0 us
  Pallas kernels: 23.1 us -> 111 us
  blocking collectives: 82.7 us -> 0 us
  between operations: 14.1 us -> 0.68 us
  matrix products: 7.95 us -> 0 us
    pallas_call x0 -> x1, Pallas kernels: none -> 92.2 us  [project(): pl.pallas_call(functools.partial(project_kernel, dp_size, mp_size), out_s...]
    all_gather x1 -> x0, waiting for transfers between devices: 74.7 us -> none  [per_device(): lax.all_gather(attended, 'dp', axis=0, tiled=True)]
    all_to_all x1 -> x0, blocking collectives: 51.1 us -> none  [per_device(): lax.all_to_all(all_rows.astype(jnp.bfloat16), 'dp', split_axis=0, concat_...]
    psum x1 -> x0, waiting for transfers between devices: 50.2 us -> none  [per_device(): lax.psum(partial_sum.astype(jnp.bfloat16), 'mp').astype(jnp.float32)]
    all_gather x1 -> x0, blocking collectives: 31.6 us -> none  [per_device(): accepted_hidden = lax.all_gather(picked_hidden, 'dp', axis=0, tiled=True)]
    dot_general x1 -> x0, matrix products: 7.95 us -> none  [per_device(): jnp.dot(lax.all_gather(attended, 'dp', axis=0, tiled=True), out_weight, p...]
    pallas_call x1, Pallas kernels: 23.1 us -> 18.6 us  [attend(): pl.pallas_call(attention_kernel, out_shape=jax.ShapeDtypeStruct(queries.s...]
    unnamed x19 -> x16, local copies, waits for them, and re-layouts: 8.55 us -> 12.3 us
  transfers between devices with their start and end apart: 2 -> 0, of which waited for: 2 -> 0; matrix products, arithmetic and copies ran while one was open for 0% -> 0% of each run, Pallas kernels for 0% -> 0%
where the time goes in v2:
time: 126 us
  Pallas kernels  111 us (88%)
  local copies, waits for them, and re-layouts  13.8 us (11%)
    pallas_call x1, Pallas kernels, project(): pl.pallas_call(functools.partial(project_kernel, dp_size, mp_size), out_s...  92.2 us
    pallas_call x1, Pallas kernels, attend(): pl.pallas_call(attention_kernel, out_shape=jax.ShapeDtypeStruct(queries.s...  18.6 us
    unnamed x16, local copies, waits for them, and re-layouts  12.3 us

profile of v2, /device:TPU:0, one launch (start us, length us, event | category | flops | bytes accessed | tf_op | source)
XLA Modules:
  0.0 126.0 jit_solution(12116169204128635971)
XLA Ops:
  0.6 0.8 broadcast_add_fusion
  1.4 0.7 reshape.13.pick_ref
  2.1 0.8 copy.12.par_ref
  2.9 0.0 copy-start
  2.9 2.2 %copy-done = bf16[2,4096,256]{2,1,0:T(8,128)(2,1)S(1)} copy-done((bf16[2,4096,256]{2,1,0:T(8,128)(2,1)S(1)}, bf16[2,4096,256]{2,1,0:T(8,128)(2,1)}, u32[]{:S(2)}) %copy-start) | copy-done | bytes 4194328
  5.0 0.0 copy-start.1
  5.0 2.2 %copy-done.1 = bf16[2,4096,256]{2,1,0:T(8,128)(2,1)S(1)} copy-done((bf16[2,4096,256]{2,1,0:T(8,128)(2,1)S(1)}, bf16[2,4096,256]{2,1,0:T(8,128)(2,1)}, u32[]{:S(2)}) %copy-start.1) | copy-done | bytes 4194328
  7.2 0.0 copy-start.3
  7.2 1.0 copy-done.3
  8.3 0.0 copy-start.4
  8.3 0.8 copy-done.4
  9.1 0.0 copy-start.5
  9.1 0.8 copy-done.5
  10.0 0.0 copy-start.6
  10.0 0.7 copy-done.6
  10.6 18.6 %attention.1.att_ref = bf16[128,2048]{1,0:T(8,128)(2,1)S(1)} custom-call(s32[2]{0:T(128)S(1)} %copy-done.6, bf16[128,2048]{1,0:T(8,128)(2,1)S(1)} %copy-done.3, bf16[128,256]{1,0:T(8,128)(2,1)S(1)} %copy-done.4, bf16[128,256]{1,0:T(8,128)(2,1)S(1)} %copy-done.5, bf16[2,4096,256]{2,1,0:T(8,128)(2,1)S(1)} %copy-done, bf16[2,4096,256]{2,1,0:T(8,128)(2,1)S(1)} %copy-done.1, ...), custom_call_target="tpu_custom_call" | custom-call | tf_op jit(solution)/shard_map/attention/pallas_call | solution.py:95
  29.2 0.0 copy-start.2
  29.2 0.8 copy-done.2
  30.0 92.2 %project.1 = (bf16[128,2048]{1,0:T(8,128)(2,1)}, bf16[128,2048]{1,0:T(8,128)(2,1)}) custom-call(bf16[128,2048]{1,0:T(8,128)(2,1)} %copy-done.2, bf16[2048,1024]{1,0:T(8,128)(2,1)} %w_ref.1, bf16[128,2048]{1,0:T(8,128)(2,1)} %res_ref.1, s32[16,1]{1,0:T(8,128)} %reshape.13.pick_ref), custom_call_target="tpu_custom_call" | custom-call | tf_op jit(solution)/shard_map/project/pallas_call | solution.py:360
  122.3 1.9 %copy.16 = bf16[128,2048]{1,0:T(8,128)(2,1)} copy(bf16[128,2048]{1,0:T(8,128)(2,1)} %get-tuple-element.4) | data formatting | bytes 1048576
  124.1 1.9 %copy.17 = bf16[128,2048]{1,0:T(8,128)(2,1)} copy(bf16[128,2048]{1,0:T(8,128)(2,1)} %get-tuple-element.5) | data formatting | bytes 1048576
  (1 shorter events, 0.0 us)
Async XLA Ops:
  2.9 2.2 %copy-start = (bf16[2,4096,256]{2,1,0:T(8,128)(2,1)S(1)}, bf16[2,4096,256]{2,1,0:T(8,128)(2,1)}, u32[]{:S(2)}) copy-start(bf16[2,4096,256]{2,1,0:T(8,128)(2,1)} %ck_ref.1) | copy-start | bytes 12582916
  5.0 2.2 %copy-start.1 = (bf16[2,4096,256]{2,1,0:T(8,128)(2,1)S(1)}, bf16[2,4096,256]{2,1,0:T(8,128)(2,1)}, u32[]{:S(2)}) copy-start(bf16[2,4096,256]{2,1,0:T(8,128)(2,1)} %cv_ref.1) | copy-start | bytes 12582916
  7.2 1.0 copy-start.3
  8.3 0.8 copy-start.4
  9.1 0.8 copy-start.5
  10.0 0.7 copy-start.6
  29.2 0.8 copy-start.2

commit v3 on v2

--- a/solution.py
+++ b/solution.py
@@ -12,6 +12,7 @@
 KV_HEADS = 8
 HD = 128
 neg_large = -1e30
+VMEM_ALL = 67043328
 MESH = pl.DeviceIdType.MESH
 
 
@@ -108,7 +109,7 @@
             ],
             out_specs=pl.BlockSpec((nodes, wide), lambda r, k, _: (r, k)),
         ),
-        compiler_params=pltpu.CompilerParams(vmem_limit_bytes=40 * 1024 * 1024),
+        compiler_params=pltpu.CompilerParams(vmem_limit_bytes=VMEM_ALL),
         name="attention",
     )(cache_lens, queries, tree_keys, tree_values, cache_keys, cache_values, parents[:, :, None])
 
@@ -125,7 +126,7 @@
     dp_size,
     mp_size,
     att_ref,
-    w_ref,
+    w_hbm,
     res_ref,
     pick_ref,
     hid_ref,
@@ -138,11 +139,11 @@
     stages = (mp_size - 1).bit_length()
     outgoing, incoming = rest[:stages], rest[stages : 2 * stages]
     (
-        settled, owned, picks,
+        w_ref, w_sem, settled, owned, picks,
         ga_send, ga_recv, st_send, st_recv, own_send, own_recv, pk_send, pk_recv,
     ) = rest[2 * stages :]
     rows = att_ref.shape[0]
-    wide = w_ref.shape[1]
+    wide = w_hbm.shape[1]
     share = dp_size // mp_size
     length = dp_size // 2
     d = lax.axis_index("dp")
@@ -150,6 +151,8 @@
     place, side = d // 2, d % 2
     peer_side = 1 - side
 
+    w_copy = pltpu.make_async_copy(w_hbm, w_ref, w_sem)
+    w_copy.start()
     barrier = pltpu.get_barrier_semaphore()
 
     def greet(i, carry):
@@ -276,6 +279,7 @@
         return own_block((k + 1) // 2) if k % 2 == 1 else peer_block(k // 2 - 1)
 
     spread(att_ref, d, place, True)
+    w_copy.wait()
     for k in range(dp_size + stages):
         if k < dp_size:
             j = block_at(k)
@@ -308,23 +312,24 @@
     ).astype(bf)
     picks[d] = picked
 
-    def pick_copy(step):
-        target = lax.rem(d + step, dp_size)
+    def pick_copy(j, way, target):
         return pltpu.make_async_remote_copy(
-            src_ref=picks.at[d],
-            dst_ref=picks.at[d],
-            send_sem=pk_send.at[step],
-            recv_sem=pk_recv.at[d],
+            src_ref=picks.at[j],
+            dst_ref=picks.at[j],
+            send_sem=pk_send.at[way],
+            recv_sem=pk_recv.at[j],
             device_id=(target, m),
             device_id_type=MESH,
         )
 
-    def pick_wait(step):
-        source = lax.rem(d + step, dp_size)
-        pltpu.make_async_copy(picks.at[source], picks.at[source], pk_recv.at[source]).wait()
-
-    for step in range(1, dp_size):
-        pick_copy(step).start()
+    peer = place * 2 + peer_side
+    pick_copy(d, 0, peer).start()
+    for e in range(1, length):
+        pick_copy(d, e, own_block(e)).start()
+    for e in range(1, length):
+        j = own_block(e)
+        pick_copy(j, length + e, peer).wait_recv()
+        pick_copy(j, length + e, peer).start()
     spread(att_ref, d, place, False)
     for e in range(1, length):
         j = own_block(e)
@@ -337,13 +342,15 @@
         def _():
             final_copy(j).wait_send()
 
-    acc_ref[pl.ds(pl.multiple_of(d * count, count), count), :] = picked
-    for step in range(1, dp_size):
-        pick_wait(step)
-        source = lax.rem(d + step, dp_size)
-        acc_ref[pl.ds(pl.multiple_of(source * count, count), count), :] = picks[source]
-    for step in range(1, dp_size):
-        pick_copy(step).wait_send()
+    for e in range(length):
+        j = peer_block(e)
+        pick_copy(j, e, peer).wait_recv()
+    for j in range(dp_size):
+        acc_ref[j * count : (j + 1) * count, :] = picks[j]
+    for e in range(length):
+        pick_copy(d, e, peer).wait_send()
+        if e:
+            pick_copy(d, length + e, peer).wait_send()
 
 
 def project(attended, out_weight, residual, picks, dp_size, mp_size):
@@ -363,13 +370,15 @@
             jax.ShapeDtypeStruct((rows, features), bf),
             jax.ShapeDtypeStruct((dp_size * count, features), bf),
         ),
-        in_specs=[vmem] * 4,
+        in_specs=[vmem, pl.BlockSpec(memory_space=pl.ANY), vmem, vmem],
         out_specs=(vmem, vmem),
         scratch_shapes=[
             pltpu.VMEM((dp_size, rows, depth), bf),
             pltpu.VMEM((dp_size, rows, wide), jnp.float32),
             *halves,
             *halves,
+            pltpu.VMEM((depth, wide), bf),
+            dma(()),
             pltpu.VMEM((dp_size, rows >> stages, wide), bf),
             pltpu.VMEM((share, mp_size, rows >> stages, wide), bf),
             pltpu.VMEM((dp_size, count, features), bf),
@@ -383,7 +392,7 @@
             dma((dp_size,)),
         ],
         compiler_params=pltpu.CompilerParams(
-            collective_id=0, has_side_effects=True, vmem_limit_bytes=56 * 1024 * 1024
+            collective_id=0, has_side_effects=True, vmem_limit_bytes=VMEM_ALL
         ),
         name="project",
     )(attended, out_weight, residual, picks)

time: 126 us -> 122 us (0.968)
  local copies, waits for them, and re-layouts: 13.8 us -> 5.85 us
  Pallas kernels: 111 us -> 114 us
    unnamed x16 -> x2, local copies, waits for them, and re-layouts: 12.3 us -> 3.76 us
    pallas_call x1, Pallas kernels: 92.2 us -> 96 us  [project(): pl.pallas_call(functools.partial(project_kernel, dp_size, mp_size), out_s...]
where the time goes in v3:
time: 122 us; the launch traced here: 121 us
  Pallas kernels  114 us (93%)
  local copies, waits for them, and re-layouts  5.85 us (5%)
    pallas_call x1, Pallas kernels, project(): pl.pallas_call(functools.partial(project_kernel, dp_size, mp_size), out_s...  96 us
    pallas_call x1, Pallas kernels, attend(): pl.pallas_call(attention_kernel, out_shape=jax.ShapeDtypeStruct(queries.s...  17.6 us
    unnamed x2, local copies, waits for them, and re-layouts  3.76 us

profile of v3, /device:TPU:0, one launch (start us, length us, event | category | flops | bytes accessed | tf_op | source)
XLA Modules:
  0.0 120.8 jit_solution(17058250671605802968)
XLA Ops:
  0.6 0.8 broadcast_add_fusion
  1.4 0.7 reshape.13.pick_ref
  2.1 1.4 %copy.12.par_ref = s32[2,64,1]{2,1,0:T(8,128)} copy(s32[2,64,1]{1,0,2:T(2,128)} %bitcast.1) | data formatting | bytes 1024 | tf_op jit(solution)/shard_map/broadcast_in_dim | solution.py:114
  3.5 17.6 %attention.1.att_ref = bf16[128,2048]{1,0:T(8,128)(2,1)} custom-call(s32[2]{0:T(128)} %lens_ref.1, bf16[128,2048]{1,0:T(8,128)(2,1)} %q_ref.1, bf16[128,256]{1,0:T(8,128)(2,1)} %tk_ref.1, bf16[128,256]{1,0:T(8,128)(2,1)} %tv_ref.1, bf16[2,4096,256]{2,1,0:T(8,128)(2,1)} %ck_ref.1, bf16[2,4096,256]{2,1,0:T(8,128)(2,1)} %cv_ref.1, s32[2,64,1]{2,1,0:T(8,128)} %copy.12.par_ref), custom_call_target="tpu_custom_call" | custom-call | tf_op jit(solution)/shard_map/attention/pallas_call | solution.py:96
  21.1 96.0 %project.1 = (bf16[128,2048]{1,0:T(8,128)(2,1)}, bf16[128,2048]{1,0:T(8,128)(2,1)}) custom-call(bf16[128,2048]{1,0:T(8,128)(2,1)} %attention.1.att_ref, bf16[2048,1024]{1,0:T(8,128)(2,1)} %w_hbm.1, bf16[128,2048]{1,0:T(8,128)(2,1)} %res_ref.1, s32[16,1]{1,0:T(8,128)} %reshape.13.pick_ref), custom_call_target="tpu_custom_call" | custom-call | tf_op jit(solution)/shard_map/project/pallas_call | solution.py:367
  117.1 1.9 %copy.16 = bf16[128,2048]{1,0:T(8,128)(2,1)} copy(bf16[128,2048]{1,0:T(8,128)(2,1)} %get-tuple-element.4) | data formatting | bytes 1048576
  118.9 1.9 %copy.17 = bf16[128,2048]{1,0:T(8,128)(2,1)} copy(bf16[128,2048]{1,0:T(8,128)(2,1)} %get-tuple-element.5) | data formatting | bytes 1048576
  (1 shorter events, 0.0 us)

commit v4 on v3

--- a/solution.py
+++ b/solution.py
@@ -16,54 +16,60 @@
 MESH = pl.DeviceIdType.MESH
 
 
-def attention_kernel(lens_ref, q_ref, tk_ref, tv_ref, ck_ref, cv_ref, par_ref, o_ref):
-    nodes = tk_ref.shape[0]
-    cache = ck_ref.shape[1]
-    group = q_ref.shape[1] // HD
-    block = min(1024, cache)
-    factor = math.log2(math.e) / math.sqrt(HD)
-    f32 = jnp.float32
-    bf = jnp.bfloat16
-    length = lens_ref[pl.program_id(0)]
-
+def ancestry(par_ref, r):
+    f32, bf = jnp.float32, jnp.bfloat16
+    nodes = par_ref.shape[1]
     lane = lax.broadcasted_iota(jnp.int32, (nodes, nodes), 1)
     row = lax.broadcasted_iota(jnp.int32, (nodes, nodes), 0)
-    reached = jnp.where((par_ref[0] == lane) | (row == lane), 1.0, 0.0).astype(f32)
+    reached = jnp.where((par_ref[r] == lane) | (row == lane), 1.0, 0.0).astype(f32)
     for _ in range((nodes - 1).bit_length()):
         hot = reached.astype(bf)
         reached = jnp.minimum(jnp.dot(hot, hot, preferred_element_type=f32), 1.0)
-
+    return reached
+
+
+def attend_unit(r, k, reached, length, q_ref, tk_ref, tv_ref, k_ref, v_ref, o_ref):
+    f32, bf = jnp.float32, jnp.bfloat16
+    nodes = reached.shape[0]
+    cache = k_ref.shape[0]
+    group = HEADS // KV_HEADS
+    block = min(1024, cache)
+    factor = math.log2(math.e) / math.sqrt(HD)
     parts = 2
     per = group // parts
-    rows = per * nodes
     nt = (((1,), (1,)), ((), ()))
+    line = slice(r * nodes, (r + 1) * nodes)
+
+    def column(p, g):
+        head = k * group + p * per + g
+        return slice(head * HD, (head + 1) * HD)
 
     def queries(p):
-        return jnp.concatenate(
-            [q_ref[:, (p * per + g) * HD : (p * per + g + 1) * HD] for g in range(per)], axis=0
-        )
+        return jnp.concatenate([q_ref[line, column(p, g)] for g in range(per)], axis=0)
 
     def with_ones(v):
         return jnp.concatenate([v, jnp.ones(v.shape, bf)], axis=1)
 
     mask = jnp.concatenate([reached] * per, axis=0) > 0.5
+    own = slice(k * HD, (k + 1) * HD)
     state = []
     for p in range(parts):
-        s = lax.dot_general(queries(p), tk_ref[...], nt, preferred_element_type=f32)
+        s = lax.dot_general(queries(p), tk_ref[line, own], nt, preferred_element_type=f32)
         s = jnp.where(mask, s, neg_large)
         m = jnp.max(s, axis=1, keepdims=True)
         w = jnp.exp2((s - m) * factor).astype(bf)
-        acc = jnp.dot(w, with_ones(tv_ref[...]), preferred_element_type=f32)
+        acc = jnp.dot(w, with_ones(tv_ref[line, own]), preferred_element_type=f32)
         state += [m, acc]
 
     def step(b, state, masked):
         start = pl.multiple_of(b * block, block)
-        k = ck_ref[0, pl.ds(start, block), :]
-        v = with_ones(cv_ref[0, pl.ds(start, block), :])
+        keys = k_ref[pl.ds(start, block), :]
+        values = with_ones(v_ref[pl.ds(start, block), :])
+        scores = [
+            lax.dot_general(queries(p), keys, nt, preferred_element_type=f32)
+            for p in range(parts)
+        ]
         out = []
-        scores = [
-            lax.dot_general(queries(p), k, nt, preferred_element_type=f32) for p in range(parts)
-        ]
         for p in range(parts):
             m, acc = state[2 * p], state[2 * p + 1]
             s = scores[p]
@@ -72,46 +78,18 @@
                 s = jnp.where(at < length, s, neg_large)
             new = jnp.maximum(m, jnp.max(s, axis=1, keepdims=True))
             w = jnp.exp2((s - new) * factor).astype(bf)
-            acc = acc * jnp.exp2((m - new) * factor) + jnp.dot(w, v, preferred_element_type=f32)
+            acc = acc * jnp.exp2((m - new) * factor) + jnp.dot(
+                w, values, preferred_element_type=f32
+            )
             out += [new, acc]
         return tuple(out)
 
-    full = length // block
-    state = lax.fori_loop(0, full, lambda b, c: step(b, c, False), tuple(state))
-    state = lax.fori_loop(full, pl.cdiv(length, block), lambda b, c: step(b, c, True), state)
+    state = lax.fori_loop(0, cache // block, lambda b, c: step(b, c, True), tuple(state))
     for p in range(parts):
         acc = state[2 * p + 1]
         done = (acc[:, :HD] / acc[:, HD:]).astype(bf)
         for g in range(per):
-            o_ref[:, (p * per + g) * HD : (p * per + g + 1) * HD] = done[
-                g * nodes : (g + 1) * nodes
-            ]
-
-
-def attend(queries, tree_keys, tree_values, cache_keys, cache_values, cache_lens, parents):
-    requests, nodes = parents.shape
-    cache = cache_keys.shape[1]
-    kv = tree_keys.shape[1] // HD
-    wide = queries.shape[1] // kv
-    return pl.pallas_call(
-        attention_kernel,
-        out_shape=jax.ShapeDtypeStruct(queries.shape, jnp.bfloat16),
-        grid_spec=pltpu.PrefetchScalarGridSpec(
-            num_scalar_prefetch=1,
-            grid=(requests, kv),
-            in_specs=[
-                pl.BlockSpec((nodes, wide), lambda r, k, _: (r, k)),
-                pl.BlockSpec((nodes, HD), lambda r, k, _: (r, k)),
-                pl.BlockSpec((nodes, HD), lambda r, k, _: (r, k)),
-                pl.BlockSpec((1, cache, HD), lambda r, k, _: (r, 0, k)),
-                pl.BlockSpec((1, cache, HD), lambda r, k, _: (r, 0, k)),
-                pl.BlockSpec((1, nodes, 1), lambda r, k, _: (r, 0, 0)),
-            ],
-            out_specs=pl.BlockSpec((nodes, wide), lambda r, k, _: (r, k)),
-        ),
-        compiler_params=pltpu.CompilerParams(vmem_limit_bytes=VMEM_ALL),
-        name="attention",
-    )(cache_lens, queries, tree_keys, tree_values, cache_keys, cache_values, parents[:, :, None])
+            o_ref[line, column(p, g)] = done[g * nodes : (g + 1) * nodes]
 
 
 def line_order(place, length, event):
@@ -125,7 +103,13 @@
 def project_kernel(
     dp_size,
     mp_size,
-    att_ref,
+    lens_ref,
+    q_ref,
+    tk_ref,
+    tv_ref,
+    ck_ref,
+    cv_ref,
+    par_ref,
     w_hbm,
     res_ref,
     pick_ref,
@@ -139,10 +123,13 @@
     stages = (mp_size - 1).bit_length()
     outgoing, incoming = rest[:stages], rest[stages : 2 * stages]
     (
-        w_ref, w_sem, settled, owned, picks,
+        att_ref, k_buf, v_buf, kv_sem, w_ref, w_sem, settled, owned, picks,
         ga_send, ga_recv, st_send, st_recv, own_send, own_recv, pk_send, pk_recv,
     ) = rest[2 * stages :]
-    rows = att_ref.shape[0]
+    rows, depth = q_ref.shape
+    requests, nodes, _ = par_ref.shape
+    units = k_buf.shape[0]
+    span = depth * requests // units
     wide = w_hbm.shape[1]
     share = dp_size // mp_size
     length = dp_size // 2
@@ -152,6 +139,16 @@
     peer_side = 1 - side
 
     w_copy = pltpu.make_async_copy(w_hbm, w_ref, w_sem)
+    loads = []
+    for c in range(units):
+        cols = slice(c // requests * HD, (c // requests + 1) * HD)
+        pair = (
+            pltpu.make_async_copy(ck_ref.at[c % requests, :, cols], k_buf.at[c], kv_sem.at[c, 0]),
+            pltpu.make_async_copy(cv_ref.at[c % requests, :, cols], v_buf.at[c], kv_sem.at[c, 1]),
+        )
+        for load in pair:
+            load.start()
+        loads.append(pair)
     w_copy.start()
     barrier = pltpu.get_barrier_semaphore()
 
@@ -167,31 +164,49 @@
     lax.fori_loop(0, dp_size * mp_size, greet, 0)
     pl.semaphore_wait(barrier, dp_size * mp_size - 1)
 
-    def gather_copy(src, j, way, target):
+    def chunk(ref, c):
+        r, k = c % requests, c // requests
+        return ref.at[r * nodes : (r + 1) * nodes, k * span : (k + 1) * span]
+
+    def gather_copy(src, j, c, way, target):
         return pltpu.make_async_remote_copy(
-            src_ref=src,
-            dst_ref=gathered.at[j],
-            send_sem=ga_send.at[j, way],
-            recv_sem=ga_recv.at[j],
+            src_ref=chunk(src, c),
+            dst_ref=chunk(gathered.at[j], c),
+            send_sem=ga_send.at[j, c, way],
+            recv_sem=ga_recv.at[j, c],
             device_id=(target, m),
             device_id_type=MESH,
         )
 
-    def spread(src, j, at, started):
-        up = place + 1
-        down = place - 1
-        for way, ok, target in (
-            (0, (at <= place) & (up < length), up * 2 + side),
-            (1, (at >= place) & (down >= 0), down * 2 + side),
-        ):
+    peer = place * 2 + peer_side
+
+    def spread(src, j, c, ways, started):
+        for way in ways:
+            target = (place + 1 - 2 * way) * 2 + side
+            ok = place < length - 1 if way == 0 else place > 0
 
             @pl.when(ok)
             def _():
-                copy = gather_copy(src, j, way, target)
+                copy = gather_copy(src, j, c, way, target)
                 copy.start() if started else copy.wait_send()
 
-        copy = gather_copy(src, j, 2, place * 2 + peer_side)
+        copy = gather_copy(src, j, c, 2, peer)
         copy.start() if started else copy.wait_send()
+
+    def relay(c, ring, started):
+        for way in range(2):
+            at = place - ring if way == 0 else place + ring
+            j = at * 2 + side
+
+            @pl.when(at >= 0 if way == 0 else at < length)
+            def _():
+                if started:
+                    gather_copy(gathered.at[j], j, c, 2, peer).wait_recv()
+                spread(gathered.at[j], j, c, (way,), started)
+
+    def slot(t):
+        for c in range(max(0, t - length + 1), min(t, units)):
+            relay(c, t - c, True)
 
     def stage_copy(t, j):
         bit = 1 << t
@@ -278,17 +293,28 @@
             return peer_block(length - 1)
         return own_block((k + 1) // 2) if k % 2 == 1 else peer_block(k // 2 - 1)
 
-    spread(att_ref, d, place, True)
+    trees = [ancestry(par_ref, r) for r in range(requests)]
+    for c in range(units):
+        r, k = c % requests, c // requests
+        for load in loads[c]:
+            load.wait()
+        attend_unit(
+            r, k, trees[r], lens_ref[r], q_ref, tk_ref, tv_ref, k_buf.at[c], v_buf.at[c], att_ref
+        )
+        spread(att_ref, d, c, (0, 1), True)
+        slot(c)
     w_copy.wait()
     for k in range(dp_size + stages):
         if k < dp_size:
             j = block_at(k)
             if k == 0:
                 multiply(att_ref, j)
+            elif k % 2 == 1 and k < dp_size - 1:
+                slot(units - 1 + (k + 1) // 2)
+                multiply(gathered.at[j], j)
             else:
-                gather_copy(gathered.at[j], j, 2, d * 0 + place * 2 + peer_side).wait_recv()
-                if k % 2 == 1 and k < dp_size - 1:
-                    spread(gathered.at[j], j, j // 2, True)
+                for c in range(units):
+                    gather_copy(gathered.at[j], j, c, 2, peer).wait_recv()
                 multiply(gathered.at[j], j)
         for t in range(stages):
             b = k - 1 - t
@@ -322,7 +348,6 @@
             device_id_type=MESH,
         )
 
-    peer = place * 2 + peer_side
     pick_copy(d, 0, peer).start()
     for e in range(1, length):
         pick_copy(d, e, own_block(e)).start()
@@ -330,10 +355,10 @@
         j = own_block(e)
         pick_copy(j, length + e, peer).wait_recv()
         pick_copy(j, length + e, peer).start()
-    spread(att_ref, d, place, False)
-    for e in range(1, length):
-        j = own_block(e)
-        spread(gathered.at[j], j, j // 2, False)
+    for c in range(units):
+        spread(att_ref, d, c, (0, 1), False)
+        for ring in range(1, length):
+            relay(c, ring, False)
     for j in range(dp_size):
         for t in range(stages):
             stage_copy(t, j).wait_send()
@@ -353,9 +378,14 @@
             pick_copy(d, length + e, peer).wait_send()
 
 
-def project(attended, out_weight, residual, picks, dp_size, mp_size):
+def project(
+    lens, queries, keys, values, cache_k, cache_v, parents, out_weight, residual, picks,
+    dp_size, mp_size,
+):
     bf = jnp.bfloat16
-    rows, depth = attended.shape
+    rows, depth = queries.shape
+    requests, cache, _ = cache_k.shape
+    units = requests * keys.shape[1] // HD
     wide = out_weight.shape[1]
     features = residual.shape[1]
     count = picks.shape[0]
@@ -364,26 +394,31 @@
     halves = [pltpu.VMEM((dp_size, rows >> (t + 1), wide), bf) for t in range(stages)]
     dma = pltpu.SemaphoreType.DMA
     vmem = pl.BlockSpec(memory_space=pltpu.VMEM)
+    hbm = pl.BlockSpec(memory_space=pl.ANY)
     return pl.pallas_call(
         functools.partial(project_kernel, dp_size, mp_size),
         out_shape=(
             jax.ShapeDtypeStruct((rows, features), bf),
             jax.ShapeDtypeStruct((dp_size * count, features), bf),
         ),
-        in_specs=[vmem, pl.BlockSpec(memory_space=pl.ANY), vmem, vmem],
+        in_specs=[pl.BlockSpec(memory_space=pltpu.SMEM), vmem, vmem, vmem, hbm, hbm, vmem, hbm, vmem, vmem],
         out_specs=(vmem, vmem),
         scratch_shapes=[
             pltpu.VMEM((dp_size, rows, depth), bf),
             pltpu.VMEM((dp_size, rows, wide), jnp.float32),
             *halves,
             *halves,
+            pltpu.VMEM((rows, depth), bf),
+            pltpu.VMEM((units, cache, HD), bf),
+            pltpu.VMEM((units, cache, HD), bf),
+            dma((units, 2)),
             pltpu.VMEM((depth, wide), bf),
             dma(()),
             pltpu.VMEM((dp_size, rows >> stages, wide), bf),
             pltpu.VMEM((share, mp_size, rows >> stages, wide), bf),
             pltpu.VMEM((dp_size, count, features), bf),
-            dma((dp_size, 3)),
-            dma((dp_size,)),
+            dma((dp_size, units, 3)),
+            dma((dp_size, units)),
             dma((stages, dp_size)),
             dma((stages, dp_size)),
             dma((dp_size,)),
@@ -395,7 +430,7 @@
             collective_id=0, has_side_effects=True, vmem_limit_bytes=VMEM_ALL
         ),
         name="project",
-    )(attended, out_weight, residual, picks)
+    )(lens, queries, keys, values, cache_k, cache_v, parents, out_weight, residual, picks)
 
 
 def per_device(
@@ -413,12 +448,12 @@
     out_weight,
 ):
     request_count, node_count = parents.shape
-    attended = attend(
-        queries, tree_keys, tree_values, cache_keys, cache_values, cache_lens, parents
-    )
     row_base = jnp.arange(request_count, dtype=jnp.int32)[:, None] * node_count
     picks = (row_base + accepted_nodes).reshape(-1, 1)
-    return project(attended, out_weight, residual, picks, dp_size, mp_size)
+    return project(
+        cache_lens, queries, tree_keys, tree_values, cache_keys, cache_values,
+        parents[:, :, None], out_weight, residual, picks, dp_size, mp_size,
+    )
 
 
 def solution(mesh):

time: 122 us -> 98.9 us (0.81)
  Pallas kernels: 114 us -> 91.1 us
    pallas_call x1 -> x0, Pallas kernels: 17.6 us -> none  [attend(): pl.pallas_call(attention_kernel, out_shape=jax.ShapeDtypeStruct(queries.s...]
    pallas_call x1, Pallas kernels: 96 us -> 91.1 us  [project(): pl.pallas_call(functools.partial(project_kernel, dp_size, mp_size), out_s...]
where the time goes in v4:
time: 98.9 us; the launch traced here: 98.4 us
  Pallas kernels  91.1 us (92%)
  local copies, waits for them, and re-layouts  5.86 us (6%)
    pallas_call x1, Pallas kernels, project(): pl.pallas_call(functools.partial(project_kernel, dp_size, mp_size), out_s...  91.1 us
    unnamed x2, local copies, waits for them, and re-layouts  3.76 us

profile of v4, /device:TPU:0, one launch (start us, length us, event | category | flops | bytes accessed | tf_op | source)
XLA Modules:
  0.0 98.4 jit_solution(12023459799841383441)
XLA Ops:
  0.6 0.8 broadcast_add_fusion
  1.4 0.7 reshape.13.pick_ref
  2.1 1.4 %copy.12.par_ref = s32[2,64,1]{2,1,0:T(8,128)} copy(s32[2,64,1]{1,0,2:T(2,128)} %bitcast.1) | data formatting | bytes 1024 | tf_op jit(solution)/shard_map/broadcast_in_dim | solution.py:455
  3.5 91.1 %project.1 = (bf16[128,2048]{1,0:T(8,128)(2,1)}, bf16[128,2048]{1,0:T(8,128)(2,1)}) custom-call(s32[2]{0:T(128)} %lens_ref.1, bf16[128,2048]{1,0:T(8,128)(2,1)} %q_ref.1, bf16[128,256]{1,0:T(8,128)(2,1)} %tk_ref.1, bf16[128,256]{1,0:T(8,128)(2,1)} %tv_ref.1, bf16[2,4096,256]{2,1,0:T(8,128)(2,1)} %ck_ref.1, bf16[2,4096,256]{2,1,0:T(8,128)(2,1)} %cv_ref.1, ...), custom_call_target="tpu_custom_call" | custom-call | tf_op jit(solution)/shard_map/project/pallas_call | solution.py:398
  94.6 1.9 %copy.16 = bf16[128,2048]{1,0:T(8,128)(2,1)} copy(bf16[128,2048]{1,0:T(8,128)(2,1)} %get-tuple-element.4) | data formatting | bytes 1048576
  96.5 1.9 %copy.17 = bf16[128,2048]{1,0:T(8,128)(2,1)} copy(bf16[128,2048]{1,0:T(8,128)(2,1)} %get-tuple-element.5) | data formatting | bytes 1048576
  (1 shorter events, 0.0 us)
